TPU v7x, 1024 devices: a whole 4x8x16 slice. The times are simulated.
1024 devices in a mesh: fsdp: 128 (over y, z_lo, x), seq: 8 (over z_hi, core).
Axes of the slice: x: 4, y: 8, z: 16 (z_hi: 4, z_lo: 4; z = z_hi * 4 + z_lo), core: 2. Of those that a mesh axis runs over, the one named last changes fastest.
Arguments:
- layer_input: bfloat16 [128, 1024, 4096], P('fsdp', 'seq'), may hold values from -24 to 24
- dt_weight: bfloat16 [4096, 64], P('fsdp'), may hold values from -0.09375 to 0.09375
- dt_bias: float32 [64], replicated, may hold values from -2 to -0.5
- decay_rate: float32 [64], replicated, may hold values from 0.0005 to 0.25
- ssm_input: bfloat16 [128, 1024, 2048], P('fsdp', 'seq'), may hold values from -6 to 6
- in_basis: bfloat16 [128, 1024, 512], P('fsdp', 'seq'), may hold values from -0.59765625 to 0.59765625
- out_basis: bfloat16 [128, 1024, 512], P('fsdp', 'seq'), may hold values from -0.59765625 to 0.59765625
- out_cotangent: bfloat16 [128, 1024, 2048], P('fsdp', 'seq'), may hold values from -6 to 6
Outputs:
- grad_input: bfloat16 [128, 1024, 2048], P('fsdp', 'seq')
- grad_in_basis: bfloat16 [128, 1024, 512], P('fsdp', 'seq')
- grad_out_basis: bfloat16 [128, 1024, 512], P('fsdp', 'seq')
- grad_dt_weight: float32 [4096, 64], P('fsdp')
All inputs are finite; a program needn't handle non-finite values.
Results may differ from a plain program's by a relative error of at most 0.011.
Values may be sent and summed in bfloat16 or wider, within the bound.
No kernel may reach another device: no remote copies, remote signals or barrier semaphores. Data moves between devices by JAX's collectives and lax.ppermute only.
A program may use at most 64 MiB of HBM per device.

v0:
```python
import jax
import jax.numpy as jnp
from jax import lax
from jax.sharding import Mesh
from jax.sharding import PartitionSpec as P


STATE = 128
LANES = 128
CORES = 2
SEQ = ("chip", "core")

HIGH = lax.Precision.HIGHEST
F32 = jnp.float32
BF16 = jnp.bfloat16


def core_swap(value):
    return lax.ppermute(value, "core", [(0, 1), (1, 0)])


def copies_to(value, axis):
    tiles = jnp.broadcast_to(value[None], (lax.axis_size(axis), *value.shape))
    return lax.all_to_all(tiles, axis, 0, 0, tiled=True)


def packed_rows(rows, packs):
    return jnp.concatenate(jnp.split(rows, packs, axis=0), axis=1)


def carried_states(forward, backward, decay, together):
    chips = lax.axis_size("chip")
    heads, head_size, _ = forward.shape
    share = heads // chips
    rows = share * head_size
    high = decay.astype(BF16)
    low = (decay - high.astype(F32)).astype(BF16)
    wide = jnp.broadcast_to(jnp.stack([high, low], axis=1)[:, :, None], (heads, 2, STATE))
    tiles = jnp.concatenate(
        [v.astype(BF16).reshape(chips, -1, STATE) for v in (forward, backward, wide)], axis=1
    )
    tiles = together(lax.all_to_all(tiles, "chip", 0, 0, tiled=True))
    shape = (chips, share, head_size, STATE)
    terms = tiles[:, :rows].reshape(shape).astype(F32)
    back = tiles[:, rows : 2 * rows].reshape(shape).astype(F32)
    factor = jnp.sum(tiles[:, 2 * rows :].reshape(chips, share, 2, STATE).astype(F32), axis=2)
    factor = factor[:, :, None, :]
    entries, laters = [jnp.zeros(shape[1:], F32)], [jnp.zeros(shape[1:], F32)]
    for i in range(chips - 1):
        entries.append(terms[i] + factor[i] * entries[-1])
        k = chips - 1 - i
        laters.append(back[k] + factor[k] * laters[-1])
    pair = jnp.stack([jnp.stack(entries), jnp.stack(laters[::-1])], axis=1)
    tiles = pair.astype(BF16).reshape(chips, 2 * rows, STATE)
    tiles = lax.all_to_all(tiles, "chip", 0, 0, tiled=True)
    return tiles[:, :rows].reshape(forward.shape), tiles[:, rows:].reshape(forward.shape)


def body(
    layer_input, dt_weight, dt_bias, decay_rate, ssm_input, in_basis, out_basis, out_cotangent
):
    upper = lax.axis_index("core") == 1

    def chosen(v, own):
        return jnp.where(upper == own, v[1], v[0])

    def in_order(own, other):
        return jnp.where(upper, jnp.stack([other, own]), jnp.stack([own, other]))

    tokens = layer_input[0]
    length, width = tokens.shape
    heads = dt_weight.shape[1] // CORES
    groups = in_basis.shape[2] // STATE // CORES
    per_group = heads // groups
    head_size = ssm_input.shape[2] // CORES // heads
    packs = LANES // heads
    rows = dt_weight.shape[0] // packs
    devices = lax.axis_size("fsdp")

    weight_half = chosen(jnp.stack(jnp.split(dt_weight, CORES, axis=1)), True)
    weight = copies_to(packed_rows(weight_half, packs), "fsdp").reshape(width // packs, LANES)
    both_tokens = jnp.stack([tokens, core_swap(tokens)]).reshape(CORES * length, width)

    def by_group(basis):
        return jnp.stack(jnp.split(basis, CORES * groups, axis=1)).reshape(CORES, -1, STATE)

    sides = [v[0].T.reshape(CORES, -1, length) for v in (ssm_input, out_cotangent)]
    sides += [by_group(v[0]) for v in (in_basis, out_basis)]
    cuts = [0]
    for side in sides:
        cuts.append(cuts[-1] + side.shape[1])
    other_sides = core_swap(jnp.concatenate([chosen(side, False) for side in sides]))
    x_half, dy_half, bin_half, bout_half = (
        in_order(chosen(side, True), other_sides[cuts[i] : cuts[i + 1]])
        for i, side in enumerate(sides)
    )
    bias, rate = (
        chosen(v.reshape(CORES, heads, 1), True) for v in (dt_bias, decay_rate)
    )

    chunk = LANES * packs
    near = rows * packs
    target = jnp.arange(chunk)
    pack, place = target // LANES, target % LANES
    source = place // rows * near + pack * rows + place % rows
    order = (jnp.arange(chunk)[:, None] == source[None, :]).astype(BF16)
    columns = jnp.einsum(
        "pgc,cad->agdp",
        both_tokens.reshape(CORES * length, width // chunk, chunk),
        order.reshape(chunk, packs, LANES),
        preferred_element_type=BF16,
    ).reshape(packs, width // packs, CORES * length)

    product = jnp.einsum("akp,km->amp", columns, weight, preferred_element_type=F32)
    raw = bias + sum(product[a, a * heads : (a + 1) * heads] for a in range(packs))
    raw = in_order(raw[:, :length], raw[:, length:])
    step_size = jax.nn.softplus(raw)
    position = jnp.arange(length)
    lower = position[:, None] >= position[None, :]
    triangle = lower.astype(F32)
    cumulative = jnp.einsum("bhu,tu->bht", -rate * step_size, triangle, precision=HIGH)
    grid = (CORES, groups, per_group, length)
    cumulative = cumulative.reshape(grid)
    final = cumulative[..., -1:]
    step_grid = step_size.reshape(grid)
    tail = jnp.exp(final - cumulative)
    leading = jnp.exp(cumulative)
    block_decay = jnp.exp(final)
    x_half = x_half.reshape(CORES, groups, per_group, head_size, length)
    dy_half = dy_half.reshape(x_half.shape)
    bin_half = bin_half.reshape(CORES, groups, length, STATE)
    bout_half = bout_half.reshape(bin_half.shape)
    inputs = x_half.astype(F32)
    upstream = dy_half.astype(F32)
    tailed = ((tail * step_grid)[..., None, :] * inputs).astype(BF16)
    led = (leading[..., None, :] * upstream).astype(BF16)
    forward = jnp.einsum("bgkps,bgsn->bgkpn", tailed, bin_half, preferred_element_type=F32)
    backward = jnp.einsum("bgkpt,bgtn->bgkpn", led, bout_half, preferred_element_type=F32)
    factor = block_decay[..., None]
    chip_forward = forward[1] + factor[1] * forward[0]
    chip_backward = backward[0] + factor[0] * backward[1]

    spread = cumulative[..., :, None] - cumulative[..., None, :]
    decay_mat = jnp.where(lower, jnp.exp(jnp.where(lower, spread, 0.0)), 0.0)
    intersection = jnp.einsum("bgtn,bgsn->bgts", bout_half, bin_half, preferred_element_type=F32)
    weighted = (decay_mat * intersection[:, :, None]).astype(BF16)
    pair = jnp.einsum("bgkpt,bgkps->bgkts", dy_half, x_half, preferred_element_type=F32)
    through = jnp.einsum("bgkpt,bgkts->bgkps", dy_half, weighted, preferred_element_type=F32)
    scaled = decay_mat * pair * step_grid[..., None, :]
    joint = jnp.sum(scaled, axis=2).astype(BF16)
    moment = scaled * intersection[:, :, None]
    change = jnp.sum(moment, axis=-1) - jnp.sum(moment, axis=-2)
    local_b = jnp.einsum("bgts,bgtn->bgsn", joint, bout_half, preferred_element_type=F32)
    local_c = jnp.einsum("bgts,bgsn->bgtn", joint, bin_half, preferred_element_type=F32)
    local = [through, change, local_b, local_c]

    def together(got):
        got, *local[:] = lax.optimization_barrier((got, *local))
        return got

    flat = (heads, head_size, STATE)
    entry, later = carried_states(
        chip_forward.reshape(flat),
        chip_backward.reshape(flat),
        (block_decay[0] * block_decay[1]).reshape(heads),
        together,
    )
    through, change, local_b, local_c = local
    entry = entry.reshape(forward.shape[1:])
    later = later.reshape(forward.shape[1:])
    entry = jnp.stack([entry, (forward[0] + factor[0] * entry).astype(BF16)])
    later = jnp.stack([(backward[1] + factor[1] * later).astype(BF16), later])

    carried = jnp.einsum("bgkpn,bgsn->bgkps", later, bin_half, preferred_element_type=F32)
    read = jnp.einsum("bgkpn,bgtn->bgkpt", entry, bout_half, preferred_element_type=F32)
    inner_x = through + tail[..., None, :] * carried
    direct = jnp.sum(inputs * inner_x, axis=3)
    entry_term = leading * jnp.sum(read * upstream, axis=3)
    exit_term = tail * step_grid * jnp.sum(inputs * carried, axis=3)
    closing = block_decay[..., 0] * jnp.sum(
        later.astype(F32) * entry.astype(F32), axis=(3, 4)
    ) + jnp.sum(exit_term, axis=-1)
    grad_cum = (change + entry_term - exit_term).reshape(CORES * heads, length)
    grad_log = jnp.dot(grad_cum, triangle, precision=HIGH).reshape(grid) + closing[..., None]
    grad_step = direct - rate.reshape(groups, per_group, 1) * grad_log
    grad_raw = grad_step.reshape(raw.shape) * jax.nn.sigmoid(raw)

    grad_raw = jnp.where(upper, grad_raw[::-1], grad_raw).astype(BF16)
    grad_raw = jnp.concatenate([grad_raw[0], grad_raw[1]], axis=1)
    zero = jnp.zeros_like(grad_raw)
    placed = jnp.stack(
        [jnp.concatenate([grad_raw if i == a else zero for i in range(packs)]) for a in range(packs)]
    )
    partial = jnp.einsum("akp,amp->km", columns, placed, preferred_element_type=F32)
    tiles = partial.astype(BF16).reshape(devices, rows, LANES)
    tiles = lax.all_to_all(tiles, "fsdp", 0, 0, tiled=True)

    grad_x = (step_grid[..., None, :] * inner_x).astype(BF16)
    grad_b = jnp.einsum("bgkps,bgkpn->bgsn", tailed, later, preferred_element_type=F32)
    grad_b = (local_b + grad_b).astype(BF16)
    grad_c = jnp.einsum("bgkpt,bgkpn->bgtn", led, entry, preferred_element_type=F32)
    grad_c = (local_c + grad_c).astype(BF16)
    outs = jnp.concatenate(
        [v.reshape(CORES, -1, LANES) for v in (grad_x, grad_b, grad_c)], axis=1
    )
    own_outs = chosen(outs, True)
    other_outs = core_swap(chosen(outs, False))

    def joined(first, last):
        return in_order(own_outs[first:last], other_outs[first:last])

    size, basis = heads * head_size, groups * length
    out_x = joined(0, size).reshape(CORES * size, length).T
    outs_bc = []
    for first in (size, size + basis):
        whole = joined(first, first + basis).reshape(CORES * groups, length, STATE)
        outs_bc.append(jnp.concatenate([whole[g] for g in range(CORES * groups)], axis=1)[None])
    own_rows = jnp.sum(tiles.astype(F32), axis=0)
    blocks = copies_to(own_rows, SEQ).reshape(-1, CORES, rows, packs, heads)
    grad_weight = jnp.sum(blocks, axis=0).transpose(2, 1, 0, 3).reshape(dt_weight.shape)
    return (out_x[None], *outs_bc, grad_weight)


def solution(mesh):
    blocks = mesh.shape["seq"]
    split = Mesh(
        mesh.devices.reshape(mesh.shape["fsdp"], blocks // CORES, CORES), ("fsdp", *SEQ)
    )
    wide = P("fsdp", SEQ, None)
    return jax.shard_map(
        body,
        mesh=split,
        in_specs=(wide, P("fsdp", None), P(), P(), wide, wide, wide, wide),
        out_specs=(wide, wide, wide, P("fsdp", None)),
        check_vma=False,
    )
```

profile of v0, /device:TPU:1, one launch (start us, length us, event | category | flops | bytes accessed | tf_op | source)
XLA Modules:
  0.0 184.7 jit_solution(1719707621368215962)
XLA Ops:
  0.7 0.9 slice_select_fusion
  1.6 0.7 broadcast_in_dim.28
  2.4 17.8 %all-to-all-start = ((bf16[128,8,128]{2,1,0:T(8,128)(2,1)}), bf16[128,8,128]{2,1,0:T(8,128)(2,1)S(1)}, u32[]{:S(2)}, u32[]{:S(2)}) async-start(bf16[128,8,128]{2,1,0:T(8,128)(2,1)} %broadcast_in_dim.28), calls=%async_computation | async-start | bytes 524288 | tf_op jit(solution)/shard_map/all_to_all | solution.py:24
  20.1 1.5 slice_bitcast_fusion.21
  21.6 1.5 slice_bitcast_fusion.14
  23.4 0.9 pad_maximum_fusion.2
  24.3 4.4 %collective-permute-start.1 = (bf16[2560,128]{0,1:T(8,128)(2,1)}, bf16[2560,128]{0,1:T(8,128)(2,1)S(1)}, u32[]{:S(2)}, u32[]{:S(2)}) collective-permute-start(bf16[2560,128]{0,1:T(8,128)(2,1)} %pad_maximum_fusion.2), channel_id=1, source_target_pairs={{0,1},{1,0},{2,3},{3,2},{4,5},{5,4},{6,7},{7,6},{8,9},{9,8},{10,11... | collective-permute-start | bytes 1966088 | tf_op jit(solution)/shard_map/ppermute | solution.py:19
  28.8 1.9 %collective-permute-start = (bf16[128,4096]{1,0:T(8,128)(2,1)S(1)}, bf16[128,4096]{1,0:T(8,128)(2,1)S(1)}, u32[]{:S(2)}, u32[]{:S(2)}) collective-permute-start(bf16[128,4096]{1,0:T(8,128)(2,1)S(1)} %bitcast.256), channel_id=1, source_target_pairs={{0,1},{1,0},{2,3},{3,2},{4,5},{5,4},{6,7},{7,6},{8,9},{9,8},{10,11... | collective-permute-start | bytes 3145736 | tf_op jit(solution)/shard_map/ppermute | solution.py:19
  30.7 0.6 fusion.66
  31.3 0.9 copy.72
  32.2 0.8 copy.68
  33.0 1.5 maximum_select_fusion.9
  34.6 0.6 broadcast_select_fusion.6
  35.2 0.7 fusion.88
  35.9 0.9 copy.67
  36.9 0.8 copy.94
  37.6 0.8 copy.71
  38.7 0.9 copy.97
  39.6 1.4 fusion.1
  42.1 0.6 slice_bitcast_fusion.32
  43.5 0.7 fusion.87
  44.3 1.4 fusion.26
  46.8 0.8 pad_maximum_fusion.3
  47.6 14.2 %all-to-all-start.1 = ((bf16[4,528,128]{2,1,0:T(8,128)(2,1)}), bf16[4,528,128]{2,1,0:T(8,128)(2,1)S(1)}, u32[]{:S(2)}, u32[]{:S(2)}) async-start(bf16[4,528,128]{2,1,0:T(8,128)(2,1)} %pad_maximum_fusion.3), calls=%async_computation.1 | async-start | bytes 1081344 | tf_op jit(solution)/shard_map/all_to_all | solution.py:42
  61.8 1.1 fusion.86
  63.0 4.5 %multiply_reduce_fusion = (f32[2,2,16,128]{3,2,1,0:T(8,128)S(1)}, f32[2,2,16,128]{3,2,1,0:T(8,128)S(1)}, bf16[2,2,128,128]{3,2,1,0:T(8,128)(2,1)S(1)}) fusion(f32[2,2,128,128]{3,2,1,0:T(8,128)S(1)} %fusion.86, f32[2,2,16,128]{3,2,1,0:T(8,128)S(1)} %get-tuple-element.20, bf16[1,2,16,32,128]{4,3,2,1,0:T(8,128)(2,1)S(1)} %bitcast.275, ...), kind=kOutput, calls=%fused_computation.3 | convolution fusion | flops 78036992 | bytes 1589249 | tf_op jit(solution)/shard_map/bgkpt,bgkps->bgkts/dot_general | solution.py:147
  67.5 0.9 fusion.44
  68.4 0.9 fusion.46
  69.4 2.8 %fusion = f32[2,2,16,32,128]{4,3,2,1,0:T(8,128)} fusion(f32[2,2,128,128]{3,2,1,0:T(8,128)S(1)} %fusion.86, f32[2,2,16,128]{3,2,1,0:T(8,128)S(1)} %bitcast.261, pred[128,128]{1,0:T(8,128)(4,1)S(1)} %iota_compare_fusion.1, bf16[1,2,16,32,128]{4,3,2,1,0:T(8,128)(2,1)S(1)} %bitcast.280, bf16[1,2,16,32,128]{4,3,2,1,0:T(8,128)(2,1)S(1)} %bitcast.290, pred[]{:T(512)S(6)} %eq.42), kind=kOutput, calls=%fused_computation.5 | convolution fusion | flops 73138176 | bytes 1884161 | tf_op jit(solution)/shard_map/bgkpt,bgkts->bgkps/dot_general | solution.py:148
  72.2 12.2 %all-to-all-done.1 = bf16[4,528,128]{2,1,0:T(8,128)(2,1)S(1)} async-done(((bf16[4,528,128]{2,1,0:T(8,128)(2,1)}), bf16[4,528,128]{2,1,0:T(8,128)(2,1)S(1)}, u32[]{:S(2)}, u32[]{:S(2)}) %all-to-all-start.1) | async-done | bytes 540704 | tf_op jit(solution)/shard_map/all_to_all | solution.py:42
  84.9 0.8 pad_maximum_fusion.4
  85.7 6.5 %all-to-all-start.2 = ((bf16[4,512,128]{2,1,0:T(8,128)(2,1)}), bf16[4,512,128]{2,1,0:T(8,128)(2,1)S(1)}, u32[]{:S(2)}, u32[]{:S(2)}) async-start(bf16[4,512,128]{2,1,0:T(8,128)(2,1)} %bitcast.72), calls=%async_computation.2 | async-start | bytes 1048576 | tf_op jit(solution)/shard_map/all_to_all | solution.py:55
  92.2 0.6 select_n.298
  93.0 13.7 %all-to-all-done.2 = bf16[4,512,128]{2,1,0:T(8,128)(2,1)S(1)} async-done(((bf16[4,512,128]{2,1,0:T(8,128)(2,1)}), bf16[4,512,128]{2,1,0:T(8,128)(2,1)S(1)}, u32[]{:S(2)}, u32[]{:S(2)}) %all-to-all-start.2) | async-done | bytes 524320 | tf_op jit(solution)/shard_map/all_to_all | solution.py:55
  106.9 1.4 fusion.9
  109.3 0.5 copy-done.10
  111.2 0.6 fusion.21
  112.7 18.2 %collective-permute-start.2 = (bf16[1536,128]{1,0:T(8,128)(2,1)S(1)}, bf16[1536,128]{1,0:T(8,128)(2,1)S(1)}, u32[]{:S(2)}, u32[]{:S(2)}) collective-permute-start(bf16[1536,128]{1,0:T(8,128)(2,1)S(1)} %get-tuple-element.29), channel_id=1, source_target_pairs={{0,1},{1,0},{2,3},{3,2},{4,5},{5,4},{6,7},{7,6},{8,9},{9,8},{10,11... | collective-permute-start | bytes 1179656 | tf_op jit(solution)/shard_map/ppermute | solution.py:19
  131.0 1.4 fusion.11
  132.4 19.6 %all-to-all-start.3 = ((bf16[128,8,128]{2,1,0:T(8,128)(2,1)}), bf16[128,8,128]{2,1,0:T(8,128)(2,1)S(1)}, u32[]{:S(2)}, u32[]{:S(2)}) async-start(bf16[128,8,128]{2,1,0:T(8,128)(2,1)} %fusion.11), calls=%async_computation.3 | async-start | bytes 524288 | tf_op jit(solution)/shard_map/all_to_all | solution.py:196
  152.2 1.0 copy.92
  153.3 0.7 maximum_bitcast_fusion.3
  154.0 11.4 %all-to-all-done.3 = bf16[128,8,128]{2,1,0:T(8,128)(2,1)S(1)} async-done(((bf16[128,8,128]{2,1,0:T(8,128)(2,1)}), bf16[128,8,128]{2,1,0:T(8,128)(2,1)S(1)}, u32[]{:S(2)}, u32[]{:S(2)}) %all-to-all-start.3) | async-done | bytes 262176 | tf_op jit(solution)/shard_map/all_to_all | solution.py:196
  165.5 0.6 broadcast_in_dim.66
  166.1 5.8 %all-to-all-start.4 = ((f32[8,8,128]{2,1,0:T(8,128)}), f32[8,8,128]{2,1,0:T(8,128)S(1)}, u32[]{:S(2)}, u32[]{:S(2)}) async-start(f32[8,8,128]{2,1,0:T(8,128)} %broadcast_in_dim.66), calls=%async_computation.4 | async-start | bytes 65536 | tf_op jit(solution)/shard_map/all_to_all | solution.py:24
  171.9 0.7 maximum_bitcast_fusion.2
  172.5 11.3 %all-to-all-done.4 = f32[8,8,128]{2,1,0:T(8,128)S(1)} async-done(((f32[8,8,128]{2,1,0:T(8,128)}), f32[8,8,128]{2,1,0:T(8,128)S(1)}, u32[]{:S(2)}, u32[]{:S(2)}) %all-to-all-start.4) | async-done | bytes 32800 | tf_op jit(solution)/shard_map/all_to_all | solution.py:24
  184.0 0.7 reshape.560
  (157 shorter events, 8.0 us)
Async XLA Ops:
  0.6 22.7 %copy-start.3 = (bf16[1,128,2048]{2,1,0:T(8,128)(2,1)S(1)}, bf16[1,128,2048]{2,1,0:T(8,128)(2,1)}, u32[]{:S(2)}) copy-start(bf16[1,128,2048]{2,1,0:T(8,128)(2,1)} %param.15) | copy-start | bytes 1572868
  0.6 22.7 %copy-start.4 = (bf16[1,128,2048]{2,1,0:T(8,128)(2,1)S(1)}, bf16[1,128,2048]{2,1,0:T(8,128)(2,1)}, u32[]{:S(2)}) copy-start(bf16[1,128,2048]{2,1,0:T(8,128)(2,1)} %param.12) | copy-start | bytes 1572868
  2.4 38.7 %all-to-all-start = ((bf16[128,8,128]{2,1,0:T(8,128)(2,1)}), bf16[128,8,128]{2,1,0:T(8,128)(2,1)S(1)}, u32[]{:S(2)}, u32[]{:S(2)}) async-start(bf16[128,8,128]{2,1,0:T(8,128)(2,1)} %broadcast_in_dim.28), calls=%async_computation | async-start | bytes 524288 | tf_op jit(solution)/shard_map/all_to_all | solution.py:24
  23.1 5.7 %copy-start.2 = (bf16[1,128,4096]{2,1,0:T(8,128)(2,1)S(1)}, bf16[1,128,4096]{2,1,0:T(8,128)(2,1)}, u32[]{:S(2)}) copy-start(bf16[1,128,4096]{2,1,0:T(8,128)(2,1)} %param.8) | copy-start | bytes 3145732
  23.3 11.2 %copy-start.29 = (f32[64]{0:T(128)S(1)}, f32[64]{0:T(128)}, u32[]{:S(2)}) copy-start(f32[64]{0:T(128)} %param.10) | copy-start | bytes 772
  23.4 11.8 %copy-start.30 = (f32[64]{0:T(128)S(1)}, f32[64]{0:T(128)}, u32[]{:S(2)}) copy-start(f32[64]{0:T(128)} %param.11) | copy-start | bytes 772
  24.3 11.5 %collective-permute-start.1 = (bf16[2560,128]{0,1:T(8,128)(2,1)}, bf16[2560,128]{0,1:T(8,128)(2,1)S(1)}, u32[]{:S(2)}, u32[]{:S(2)}) collective-permute-start(bf16[2560,128]{0,1:T(8,128)(2,1)} %pad_maximum_fusion.2), channel_id=1, source_target_pairs={{0,1},{1,0},{2,3},{3,2},{4,5},{5,4},{6,7},{7,6},{8,9},{9,8},{10,11... | collective-permute-start | bytes 1966088 | tf_op jit(solution)/shard_map/ppermute | solution.py:19
  28.8 9.7 %collective-permute-start = (bf16[128,4096]{1,0:T(8,128)(2,1)S(1)}, bf16[128,4096]{1,0:T(8,128)(2,1)S(1)}, u32[]{:S(2)}, u32[]{:S(2)}) collective-permute-start(bf16[128,4096]{1,0:T(8,128)(2,1)S(1)} %bitcast.256), channel_id=1, source_target_pairs={{0,1},{1,0},{2,3},{3,2},{4,5},{5,4},{6,7},{7,6},{8,9},{9,8},{10,11... | collective-permute-start | bytes 3145736 | tf_op jit(solution)/shard_map/ppermute | solution.py:19
  38.7 0.9 copy-start.28
  41.0 3.2 %copy-start = (bf16[4,128,256,8]{2,1,3,0:T(8,128)(2,1)}, bf16[4,128,256,8]{2,1,3,0:T(8,128)(2,1)S(1)}, u32[]{:S(2)}) copy-start(bf16[4,128,256,8]{2,1,3,0:T(8,128)(2,1)S(1)} %fusion.1) | copy-start | bytes 6291460
  41.0 0.6 copy-start.27
  41.0 0.7 copy-start.33
  41.0 3.2 %copy-start.5 = (bf16[1024,128]{1,0:T(8,128)(2,1)S(1)}, bf16[1024,128]{1,0:T(8,128)(2,1)}, u32[]{:S(2)}) copy-start(bf16[1024,128]{1,0:T(8,128)(2,1)} %copy.68) | copy-start | bytes 786436
  42.1 2.1 %copy-start.18 = (f32[2,2,16,1]{2,1,0,3:T(2,128)}, f32[2,2,16,1]{2,1,0,3:T(2,128)S(1)}, u32[]{:S(2)}) copy-start(f32[2,2,16,1]{2,1,0,3:T(2,128)S(1)} %copy.96) | copy-start | bytes 772
  44.2 1.6 copy-start.23
  44.2 18.7 %copy-start.20 = (f32[2,2,16,128]{3,2,1,0:T(8,128)}, f32[2,2,16,128]{3,2,1,0:T(8,128)S(1)}, u32[]{:S(2)}) copy-start(f32[2,2,16,128]{3,2,1,0:T(8,128)S(1)} %get-tuple-element.20) | copy-start | bytes 98308
  44.2 1.6 copy-start.6
  44.3 1.6 copy-start.8
  44.3 1.6 copy-start.11
  44.3 1.6 copy-start.15
  46.3 15.5 %copy-start.13 = (bf16[1,2,128,128]{3,2,1,0:T(8,128)(2,1)S(1)}, bf16[1,2,128,128]{3,2,1,0:T(8,128)(2,1)}, u32[]{:S(2)}) copy-start(bf16[1,2,128,128]{3,2,1,0:T(8,128)(2,1)} %get-tuple-element.116) | copy-start | bytes 196612
  47.6 36.8 %all-to-all-start.1 = ((bf16[4,528,128]{2,1,0:T(8,128)(2,1)}), bf16[4,528,128]{2,1,0:T(8,128)(2,1)S(1)}, u32[]{:S(2)}, u32[]{:S(2)}) async-start(bf16[4,528,128]{2,1,0:T(8,128)(2,1)} %pad_maximum_fusion.3), calls=%async_computation.1 | async-start | bytes 1081344 | tf_op jit(solution)/shard_map/all_to_all | solution.py:42
  62.9 5.5 %copy-start.16 = (bf16[1,2,128,128]{3,2,1,0:T(8,128)(2,1)S(1)}, bf16[1,2,128,128]{3,2,1,0:T(8,128)(2,1)}, u32[]{:S(2)}) copy-start(bf16[1,2,128,128]{3,2,1,0:T(8,128)(2,1)} %get-tuple-element.117) | copy-start | bytes 196612
  63.0 6.4 %copy-start.9 = (bf16[1024,128]{1,0:T(8,128)(2,1)S(1)}, bf16[1024,128]{1,0:T(8,128)(2,1)}, u32[]{:S(2)}) copy-start(bf16[1024,128]{1,0:T(8,128)(2,1)} %copy.71) | copy-start | bytes 786436
  84.6 8.3 %copy-start.19 = (f32[2,2,16,1]{2,1,0,3:T(2,128)S(1)}, f32[2,2,16,1]{2,1,0,3:T(2,128)}, u32[]{:S(2)}) copy-start(f32[2,2,16,1]{2,1,0,3:T(2,128)} %copy-done.18) | copy-start | bytes 772
  84.7 7.5 %copy-start.32 = (f32[32]{0:T(128)S(1)}, f32[32]{0:T(128)}, u32[]{:S(2)}) copy-start(f32[32]{0:T(128)} %get-tuple-element.23) | copy-start | bytes 388
  84.7 22.0 %copy-start.26 = (f32[2,16]{1,0:T(2,128)S(1)}, f32[2,16]{1,0:T(2,128)}, u32[]{:S(2)}) copy-start(f32[2,16]{1,0:T(2,128)} %get-tuple-element.109) | copy-start | bytes 388
  84.8 22.0 %copy-start.12 = (bf16[256,128]{1,0:T(8,128)(2,1)S(1)}, bf16[256,128]{1,0:T(8,128)(2,1)}, u32[]{:S(2)}) copy-start(bf16[256,128]{1,0:T(8,128)(2,1)} %copy.94) | copy-start | bytes 196612
  84.8 22.0 %copy-start.17 = (bf16[1,2,128,128]{3,2,1,0:T(8,128)(2,1)S(1)}, bf16[1,2,128,128]{3,2,1,0:T(8,128)(2,1)}, u32[]{:S(2)}) copy-start(bf16[1,2,128,128]{3,2,1,0:T(8,128)(2,1)} %get-tuple-element.117) | copy-start | bytes 196612
  85.7 21.0 %all-to-all-start.2 = ((bf16[4,512,128]{2,1,0:T(8,128)(2,1)}), bf16[4,512,128]{2,1,0:T(8,128)(2,1)S(1)}, u32[]{:S(2)}, u32[]{:S(2)}) async-start(bf16[4,512,128]{2,1,0:T(8,128)(2,1)} %bitcast.72), calls=%async_computation.2 | async-start | bytes 1048576 | tf_op jit(solution)/shard_map/all_to_all | solution.py:55
  106.9 1.5 copy-start.25
  106.9 1.9 %copy-start.7 = (bf16[1024,128]{1,0:T(8,128)(2,1)S(1)}, bf16[1024,128]{1,0:T(8,128)(2,1)}, u32[]{:S(2)}) copy-start(bf16[1024,128]{1,0:T(8,128)(2,1)} %copy.67) | copy-start | bytes 786436
  106.9 1.9 %copy-start.34 = (f32[2,2,128,128]{3,2,1,0:T(8,128)S(1)}, f32[2,2,128,128]{3,2,1,0:T(8,128)}, u32[]{:S(2)}) copy-start(f32[2,2,128,128]{3,2,1,0:T(8,128)} %fusion.46) | copy-start | bytes 786436
  108.8 1.0 copy-start.10
  108.8 0.9 copy-start.24
  108.8 1.0 copy-start.35
  109.9 0.8 copy-start.14
  109.9 0.8 copy-start.21
  109.9 0.8 copy-start.22
  109.9 1.3 copy-start.36
  111.8 0.7 copy-start.31
  111.8 19.2 %copy-start.1 = (bf16[4,128,256,8]{2,1,3,0:T(8,128)(2,1)S(1)}, bf16[4,128,256,8]{2,1,3,0:T(8,128)(2,1)}, u32[]{:S(2)}) copy-start(bf16[4,128,256,8]{2,1,3,0:T(8,128)(2,1)} %copy-done) | copy-start | bytes 6291460
  112.7 39.3 %collective-permute-start.2 = (bf16[1536,128]{1,0:T(8,128)(2,1)S(1)}, bf16[1536,128]{1,0:T(8,128)(2,1)S(1)}, u32[]{:S(2)}, u32[]{:S(2)}) collective-permute-start(bf16[1536,128]{1,0:T(8,128)(2,1)S(1)} %get-tuple-element.29), channel_id=1, source_target_pairs={{0,1},{1,0},{2,3},{3,2},{4,5},{5,4},{6,7},{7,6},{8,9},{9,8},{10,11... | collective-permute-start | bytes 1179656 | tf_op jit(solution)/shard_map/ppermute | solution.py:19
  132.4 32.9 %all-to-all-start.3 = ((bf16[128,8,128]{2,1,0:T(8,128)(2,1)}), bf16[128,8,128]{2,1,0:T(8,128)(2,1)S(1)}, u32[]{:S(2)}, u32[]{:S(2)}) async-start(bf16[128,8,128]{2,1,0:T(8,128)(2,1)} %fusion.11), calls=%async_computation.3 | async-start | bytes 524288 | tf_op jit(solution)/shard_map/all_to_all | solution.py:196
  166.1 17.7 %all-to-all-start.4 = ((f32[8,8,128]{2,1,0:T(8,128)}), f32[8,8,128]{2,1,0:T(8,128)S(1)}, u32[]{:S(2)}, u32[]{:S(2)}) async-start(f32[8,8,128]{2,1,0:T(8,128)} %broadcast_in_dim.66), calls=%async_computation.4 | async-start | bytes 65536 | tf_op jit(solution)/shard_map/all_to_all | solution.py:24
where the time goes:
time: 186 us; the launch traced here: 185 us
  starting transfers between devices  88.4 us (48%)
  waiting for transfers between devices  48.6 us (26%)
  matrix products  18.7 us (10%)
  local copies, waits for them, and re-layouts  15.7 us (8%)
  other arithmetic  11.9 us (6%)
    ppermute x3, starting transfers between devices, core_swap(): return lax.ppermute(value, 'core', [(0, 1), (1, 0)])  24.6 us
    all_to_all x2, starting transfers between devices, copies_to(): return lax.all_to_all(tiles, axis, 0, 0, tiled=True)  23.5 us
    all_to_all x1, starting transfers between devices, body(): tiles = lax.all_to_all(tiles, 'fsdp', 0, 0, tiled=True)  19.6 us
    all_to_all x1, starting transfers between devices, carried_states(): tiles = together(lax.all_to_all(tiles, 'chip', 0, 0, tiled=True))  14.2 us
    all_to_all x1, waiting for transfers between devices, carried_states(): tiles = lax.all_to_all(tiles, 'chip', 0, 0, tiled=True)  13.7 us
    all_to_all x1, waiting for transfers between devices, carried_states(): tiles = together(lax.all_to_all(tiles, 'chip', 0, 0, tiled=True))  12.2 us
    all_to_all x1, waiting for transfers between devices, body(): tiles = lax.all_to_all(tiles, 'fsdp', 0, 0, tiled=True)  11.4 us
    all_to_all x2, waiting for transfers between devices, copies_to(): return lax.all_to_all(tiles, axis, 0, 0, tiled=True)  11.3 us
  transfers between devices with their start and end apart: 8, of which 4 were waited for; matrix products, arithmetic and copies ran while one was open for 16% of the time, Pallas kernels for 0%

commit v1 on v0

--- a/solution.py
+++ b/solution.py
@@ -33,18 +33,18 @@
     heads, head_size, _ = forward.shape
     share = heads // chips
     rows = share * head_size
-    high = decay.astype(BF16)
-    low = (decay - high.astype(F32)).astype(BF16)
-    wide = jnp.broadcast_to(jnp.stack([high, low], axis=1)[:, :, None], (heads, 2, STATE))
+    wide = jnp.broadcast_to(decay[:, None], (heads, STATE))
+    high = wide.astype(BF16)
+    low = wide - high.astype(F32)
     tiles = jnp.concatenate(
-        [v.astype(BF16).reshape(chips, -1, STATE) for v in (forward, backward, wide)], axis=1
+        [v.astype(BF16).reshape(chips, -1, STATE) for v in (forward, backward, high, low)], axis=1
     )
     tiles = together(lax.all_to_all(tiles, "chip", 0, 0, tiled=True))
     shape = (chips, share, head_size, STATE)
     terms = tiles[:, :rows].reshape(shape).astype(F32)
     back = tiles[:, rows : 2 * rows].reshape(shape).astype(F32)
-    factor = jnp.sum(tiles[:, 2 * rows :].reshape(chips, share, 2, STATE).astype(F32), axis=2)
-    factor = factor[:, :, None, :]
+    factors = tiles[:, 2 * rows :].astype(F32)
+    factor = (factors[:, :share] + factors[:, share:])[:, :, None, :]
     entries, laters = [jnp.zeros(shape[1:], F32)], [jnp.zeros(shape[1:], F32)]
     for i in range(chips - 1):
         entries.append(terms[i] + factor[i] * entries[-1])
@@ -81,19 +81,31 @@
     weight = copies_to(packed_rows(weight_half, packs), "fsdp").reshape(width // packs, LANES)
     both_tokens = jnp.stack([tokens, core_swap(tokens)]).reshape(CORES * length, width)
 
-    def by_group(basis):
-        return jnp.stack(jnp.split(basis, CORES * groups, axis=1)).reshape(CORES, -1, STATE)
-
-    sides = [v[0].T.reshape(CORES, -1, length) for v in (ssm_input, out_cotangent)]
-    sides += [by_group(v[0]) for v in (in_basis, out_basis)]
+    sides = [v[0] for v in (ssm_input, out_cotangent, in_basis, out_basis)]
     cuts = [0]
     for side in sides:
-        cuts.append(cuts[-1] + side.shape[1])
-    other_sides = core_swap(jnp.concatenate([chosen(side, False) for side in sides]))
+        cuts.append(cuts[-1] + side.shape[1] // CORES)
+
+    def picked(v, own):
+        low, high = jnp.split(v, CORES, axis=1)
+        return jnp.where(upper == own, high, low)
+
+    other_sides = core_swap(jnp.concatenate([picked(side, False) for side in sides], axis=1))
     x_half, dy_half, bin_half, bout_half = (
-        in_order(chosen(side, True), other_sides[cuts[i] : cuts[i + 1]])
+        (picked(side, True), other_sides[:, cuts[i] : cuts[i + 1]])
         for i, side in enumerate(sides)
     )
+
+    def tiled(pair):
+        return in_order(*(jnp.stack(jnp.split(v, v.shape[1] // LANES, axis=1)) for v in pair))
+
+    unit = jnp.eye(heads * head_size, dtype=BF16)
+
+    def turned(pair):
+        return jnp.einsum("bsc,cd->bds", in_order(*pair), unit, preferred_element_type=BF16)
+
+    x_half, dy_half = turned(x_half), turned(dy_half)
+    bin_half, bout_half = tiled(bin_half), tiled(bout_half)
     bias, rate = (
         chosen(v.reshape(CORES, heads, 1), True) for v in (dt_bias, decay_rate)
     )
@@ -162,7 +174,7 @@
     entry, later = carried_states(
         chip_forward.reshape(flat),
         chip_backward.reshape(flat),
-        (block_decay[0] * block_decay[1]).reshape(heads),
+        jnp.exp(final[0] + final[1]).reshape(heads),
         together,
     )
     through, change, local_b, local_c = local
@@ -179,9 +191,11 @@
     exit_term = tail * step_grid * jnp.sum(inputs * carried, axis=3)
     closing = block_decay[..., 0] * jnp.sum(
         later.astype(F32) * entry.astype(F32), axis=(3, 4)
-    ) + jnp.sum(exit_term, axis=-1)
-    grad_cum = (change + entry_term - exit_term).reshape(CORES * heads, length)
-    grad_log = jnp.dot(grad_cum, triangle, precision=HIGH).reshape(grid) + closing[..., None]
+    )
+    grad_cum = jnp.concatenate([change + entry_term, exit_term], axis=-1)
+    sums = jnp.concatenate([triangle, 1.0 - triangle])
+    grad_log = jnp.dot(grad_cum.reshape(CORES * heads, -1), sums, precision=HIGH)
+    grad_log = grad_log.reshape(grid) + closing[..., None]
     grad_step = direct - rate.reshape(groups, per_group, 1) * grad_log
     grad_raw = grad_step.reshape(raw.shape) * jax.nn.sigmoid(raw)
 

time: 186 us -> 181 us (0.973)
  local copies, waits for them, and re-layouts: 15.7 us -> 8.5 us
  other arithmetic: 11.9 us -> 14.5 us
    another operation x2 -> x6, other arithmetic: 0.11 us -> 3.27 us  [the longest x5 3.17 us: in_order(): return jnp.where(upper, jnp.stack([other, own]), jnp.stack([own, other]))]
    another operation x5, local copies, waits for them, and re-layouts: 3.06 us -> 0.06 us  [the longest x3 0.04 us: tiled(): jnp.stack(jnp.split(v, v.shape[1] // LANES, axis=1))]
    select_n x5 -> x1, local copies, waits for them, and re-layouts: 2.56 us -> 0.08 us  [chosen(): return jnp.where(upper == own, v[1], v[0])]
    select_n x6 -> x3, other arithmetic: 3.17 us -> 0.98 us  [chosen(): return jnp.where(upper == own, v[1], v[0])]
  transfers between devices with their start and end apart: 8 -> 8, of which waited for: 4 -> 4; matrix products, arithmetic and copies ran while one was open for 16% -> 13% of each run, Pallas kernels for 0% -> 0%
where the time goes in v1:
time: 181 us; the launch traced here: 180 us
  starting transfers between devices  88.4 us (49%)
  waiting for transfers between devices  48.5 us (27%)
  matrix products  18.5 us (10%)
  other arithmetic  14.5 us (8%)
  local copies, waits for them, and re-layouts  8.5 us (5%)
    ppermute x3, starting transfers between devices, core_swap(): return lax.ppermute(value, 'core', [(0, 1), (1, 0)])  24.6 us
    all_to_all x2, starting transfers between devices, copies_to(): return lax.all_to_all(tiles, axis, 0, 0, tiled=True)  23.5 us
    all_to_all x1, starting transfers between devices, body(): tiles = lax.all_to_all(tiles, 'fsdp', 0, 0, tiled=True)  19.6 us
    all_to_all x1, starting transfers between devices, carried_states(): tiles = together(lax.all_to_all(tiles, 'chip', 0, 0, tiled=True))  14.2 us
    all_to_all x1, waiting for transfers between devices, carried_states(): tiles = lax.all_to_all(tiles, 'chip', 0, 0, tiled=True)  13.1 us
    all_to_all x1, waiting for transfers between devices, carried_states(): tiles = together(lax.all_to_all(tiles, 'chip', 0, 0, tiled=True))  12.7 us
    all_to_all x1, waiting for transfers between devices, body(): tiles = lax.all_to_all(tiles, 'fsdp', 0, 0, tiled=True)  11.4 us
    all_to_all x2, waiting for transfers between devices, copies_to(): return lax.all_to_all(tiles, axis, 0, 0, tiled=True)  11.3 us
  transfers between devices with their start and end apart: 8, of which 4 were waited for; matrix products, arithmetic and copies ran while one was open for 13% of the time, Pallas kernels for 0%

profile of v1, /device:TPU:1, one launch (start us, length us, event | category | flops | bytes accessed | tf_op | source)
XLA Modules:
  0.0 179.8 jit_solution(15552786097352339633)
XLA Ops:
  0.6 0.8 slice_select_fusion
  1.6 0.8 broadcast_in_dim.28
  2.3 17.8 %all-to-all-start = ((bf16[128,8,128]{2,1,0:T(8,128)(2,1)}), bf16[128,8,128]{2,1,0:T(8,128)(2,1)S(1)}, u32[]{:S(2)}, u32[]{:S(2)}) async-start(bf16[128,8,128]{2,1,0:T(8,128)(2,1)} %broadcast_in_dim.28), calls=%async_computation | async-start | bytes 524288 | tf_op jit(solution)/shard_map/all_to_all | solution.py:24
  20.1 1.0 broadcast_select_fusion.3
  21.2 1.3 select_bitcast_fusion.2
  22.5 4.4 %collective-permute-start.1 = (bf16[128,2560]{1,0:T(8,128)(2,1)S(1)}, bf16[128,2560]{1,0:T(8,128)(2,1)S(1)}, u32[]{:S(2)}, u32[]{:S(2)}) collective-permute-start(bf16[128,2560]{1,0:T(8,128)(2,1)S(1)} %pad_maximum_fusion.2), channel_id=1, source_target_pairs={{0,1},{1,0},{2,3},{3,2},{4,5},{5,4},{6,7},{7,6},{8,9},{9,8},{10,11... | collective-permute-start | bytes 1966088 | tf_op jit(solution)/shard_map/ppermute | solution.py:19
  27.0 1.9 %collective-permute-start = (bf16[128,4096]{1,0:T(8,128)(2,1)S(1)}, bf16[128,4096]{1,0:T(8,128)(2,1)S(1)}, u32[]{:S(2)}, u32[]{:S(2)}) collective-permute-start(bf16[128,4096]{1,0:T(8,128)(2,1)S(1)} %bitcast.240), channel_id=1, source_target_pairs={{0,1},{1,0},{2,3},{3,2},{4,5},{5,4},{6,7},{7,6},{8,9},{9,8},{10,11... | collective-permute-start | bytes 3145736 | tf_op jit(solution)/shard_map/ppermute | solution.py:19
  28.9 0.6 maximum_bitcast_fusion.9
  29.6 0.6 fusion.117
  30.3 0.6 maximum_bitcast_fusion.6
  31.0 0.8 fusion.3
  31.8 0.6 maximum_bitcast_fusion.8
  32.4 0.8 fusion.1
  33.4 0.9 copy.48
  34.3 1.4 fusion.6
  35.8 0.5 convolution_bitcast_fusion.1
  37.0 0.6 subtract_convert_fusion
  37.9 0.7 mul.270
  38.7 0.7 mul.263
  39.3 0.7 fusion.116
  40.0 1.2 fusion.43
  41.3 1.2 fusion.46
  43.6 0.8 pad_maximum_fusion.3
  44.5 14.2 %all-to-all-start.1 = ((bf16[4,528,128]{2,1,0:T(8,128)(2,1)}), bf16[4,528,128]{2,1,0:T(8,128)(2,1)S(1)}, u32[]{:S(2)}, u32[]{:S(2)}) async-start(bf16[4,528,128]{2,1,0:T(8,128)(2,1)} %pad_maximum_fusion.3), calls=%async_computation.1 | async-start | bytes 1081344 | tf_op jit(solution)/shard_map/all_to_all | solution.py:42
  58.9 4.3 %multiply_reduce_fusion = (f32[2,2,16,128]{3,2,1,0:T(8,128)S(1)}, f32[2,2,16,128]{3,2,1,0:T(8,128)S(1)}, bf16[2,2,128,128]{3,2,1,0:T(8,128)(2,1)S(1)}) fusion(f32[2,2,128,128]{3,2,1,0:T(8,128)S(1)} %fusion.115, f32[2,2,16,128]{3,2,1,0:T(8,128)} %get-tuple-element.22, bf16[2,2,16,32,128]{4,3,2,1,0:T(8,128)(2,1)} %bitcast.252, ...), kind=kOutput, calls=%fused_computation.7 | convolution fusion | flops 76464128 | bytes 1589248 | tf_op jit(solution)/shard_map/bgkpt,bgkps->bgkts/dot_general | solution.py:159
  63.2 0.6 sub.66
  63.8 0.9 fusion.66
  64.7 0.9 fusion.68
  65.7 2.8 %fusion.5 = f32[2,2,16,32,128]{4,3,2,1,0:T(8,128)} fusion(bf16[2,2,16,32,128]{4,3,2,1,0:T(8,128)(2,1)S(1)} %bitcast.253, f32[2,2,128,128]{3,2,1,0:T(8,128)S(1)} %fusion.115, f32[2,2,16,128]{3,2,1,0:T(8,128)S(1)} %bitcast.245, pred[128,128]{1,0:T(8,128)(4,1)S(1)} %iota_compare_fusion.2), kind=kOutput, calls=%fused_computation.9 | convolution fusion | flops 72351744 | bytes 1884160 | tf_op jit(solution)/shard_map/bgkpt,bgkts->bgkps/dot_general | solution.py:160
  68.5 12.7 %all-to-all-done.1 = bf16[4,528,128]{2,1,0:T(8,128)(2,1)S(1)} async-done(((bf16[4,528,128]{2,1,0:T(8,128)(2,1)}), bf16[4,528,128]{2,1,0:T(8,128)(2,1)S(1)}, u32[]{:S(2)}, u32[]{:S(2)}) %all-to-all-start.1) | async-done | bytes 540704 | tf_op jit(solution)/shard_map/all_to_all | solution.py:42
  81.6 0.8 pad_maximum_fusion.4
  82.5 6.5 %all-to-all-start.2 = ((bf16[4,512,128]{2,1,0:T(8,128)(2,1)}), bf16[4,512,128]{2,1,0:T(8,128)(2,1)S(1)}, u32[]{:S(2)}, u32[]{:S(2)}) async-start(bf16[4,512,128]{2,1,0:T(8,128)(2,1)} %bitcast.66), calls=%async_computation.2 | async-start | bytes 1048576 | tf_op jit(solution)/shard_map/all_to_all | solution.py:55
  89.1 0.6 broadcast_subtract_fusion
  89.7 0.6 fusion.74
  90.4 13.1 %all-to-all-done.2 = bf16[4,512,128]{2,1,0:T(8,128)(2,1)S(1)} async-done(((bf16[4,512,128]{2,1,0:T(8,128)(2,1)}), bf16[4,512,128]{2,1,0:T(8,128)(2,1)S(1)}, u32[]{:S(2)}, u32[]{:S(2)}) %all-to-all-start.2) | async-done | bytes 524320 | tf_op jit(solution)/shard_map/all_to_all | solution.py:55
  103.8 0.7 copy-done.5
  106.4 0.6 fusion.26
  107.8 18.2 %collective-permute-start.2 = (bf16[1536,128]{1,0:T(8,128)(2,1)S(1)}, bf16[1536,128]{1,0:T(8,128)(2,1)S(1)}, u32[]{:S(2)}, u32[]{:S(2)}) collective-permute-start(bf16[1536,128]{1,0:T(8,128)(2,1)S(1)} %get-tuple-element.33), channel_id=1, source_target_pairs={{0,1},{1,0},{2,3},{3,2},{4,5},{5,4},{6,7},{7,6},{8,9},{9,8},{10,11... | collective-permute-start | bytes 1179656 | tf_op jit(solution)/shard_map/ppermute | solution.py:19
  126.1 1.4 fusion.16
  127.5 19.6 %all-to-all-start.3 = ((bf16[128,8,128]{2,1,0:T(8,128)(2,1)}), bf16[128,8,128]{2,1,0:T(8,128)(2,1)S(1)}, u32[]{:S(2)}, u32[]{:S(2)}) async-start(bf16[128,8,128]{2,1,0:T(8,128)(2,1)} %fusion.16), calls=%async_computation.3 | async-start | bytes 524288 | tf_op jit(solution)/shard_map/all_to_all | solution.py:210
  147.3 1.0 copy.46
  148.4 0.7 maximum_bitcast_fusion.3
  149.1 11.4 %all-to-all-done.3 = bf16[128,8,128]{2,1,0:T(8,128)(2,1)S(1)} async-done(((bf16[128,8,128]{2,1,0:T(8,128)(2,1)}), bf16[128,8,128]{2,1,0:T(8,128)(2,1)S(1)}, u32[]{:S(2)}, u32[]{:S(2)}) %all-to-all-start.3) | async-done | bytes 262176 | tf_op jit(solution)/shard_map/all_to_all | solution.py:210
  160.6 0.6 broadcast_in_dim.65
  161.2 5.8 %all-to-all-start.4 = ((f32[8,8,128]{2,1,0:T(8,128)}), f32[8,8,128]{2,1,0:T(8,128)S(1)}, u32[]{:S(2)}, u32[]{:S(2)}) async-start(f32[8,8,128]{2,1,0:T(8,128)} %broadcast_in_dim.65), calls=%async_computation.4 | async-start | bytes 65536 | tf_op jit(solution)/shard_map/all_to_all | solution.py:24
  166.9 0.7 maximum_bitcast_fusion.2
  167.6 11.3 %all-to-all-done.4 = f32[8,8,128]{2,1,0:T(8,128)S(1)} async-done(((f32[8,8,128]{2,1,0:T(8,128)}), f32[8,8,128]{2,1,0:T(8,128)S(1)}, u32[]{:S(2)}, u32[]{:S(2)}) %all-to-all-start.4) | async-done | bytes 32800 | tf_op jit(solution)/shard_map/all_to_all | solution.py:24
  179.1 0.7 reshape.414
  (139 shorter events, 6.7 us)
Async XLA Ops:
  2.3 33.4 %all-to-all-start = ((bf16[128,8,128]{2,1,0:T(8,128)(2,1)}), bf16[128,8,128]{2,1,0:T(8,128)(2,1)S(1)}, u32[]{:S(2)}, u32[]{:S(2)}) async-start(bf16[128,8,128]{2,1,0:T(8,128)(2,1)} %broadcast_in_dim.28), calls=%async_computation | async-start | bytes 524288 | tf_op jit(solution)/shard_map/all_to_all | solution.py:24
  20.1 6.9 %copy-start.2 = (bf16[1,128,4096]{2,1,0:T(8,128)(2,1)S(1)}, bf16[1,128,4096]{2,1,0:T(8,128)(2,1)}, u32[]{:S(2)}) copy-start(bf16[1,128,4096]{2,1,0:T(8,128)(2,1)} %param.8) | copy-start | bytes 3145732
  21.1 8.4 %copy-start.24 = (f32[64]{0:T(128)S(1)}, f32[64]{0:T(128)}, u32[]{:S(2)}) copy-start(f32[64]{0:T(128)} %param.10) | copy-start | bytes 772
  21.2 8.5 %copy-start.25 = (f32[64]{0:T(128)S(1)}, f32[64]{0:T(128)}, u32[]{:S(2)}) copy-start(f32[64]{0:T(128)} %param.11) | copy-start | bytes 772
  22.5 7.8 %collective-permute-start.1 = (bf16[128,2560]{1,0:T(8,128)(2,1)S(1)}, bf16[128,2560]{1,0:T(8,128)(2,1)S(1)}, u32[]{:S(2)}, u32[]{:S(2)}) collective-permute-start(bf16[128,2560]{1,0:T(8,128)(2,1)S(1)} %pad_maximum_fusion.2), channel_id=1, source_target_pairs={{0,1},{1,0},{2,3},{3,2},{4,5},{5,4},{6,7},{7,6},{8,9},{9,8},{10,11... | collective-permute-start | bytes 1966088 | tf_op jit(solution)/shard_map/ppermute | solution.py:19
  27.0 6.3 %collective-permute-start = (bf16[128,4096]{1,0:T(8,128)(2,1)S(1)}, bf16[128,4096]{1,0:T(8,128)(2,1)S(1)}, u32[]{:S(2)}, u32[]{:S(2)}) collective-permute-start(bf16[128,4096]{1,0:T(8,128)(2,1)S(1)} %bitcast.240), channel_id=1, source_target_pairs={{0,1},{1,0},{2,3},{3,2},{4,5},{5,4},{6,7},{7,6},{8,9},{9,8},{10,11... | collective-permute-start | bytes 3145736 | tf_op jit(solution)/shard_map/ppermute | solution.py:19
  33.2 8.1 %copy-start.3 = (bf16[1024,2,128]{2,0,1:T(8,128)(2,1)}, bf16[1024,2,128]{2,0,1:T(8,128)(2,1)S(1)}, u32[]{:S(2)}) copy-start(bf16[1024,2,128]{2,0,1:T(8,128)(2,1)S(1)} %fusion.1) | copy-start | bytes 1572868
  35.7 4.3 %copy-start = (bf16[4,128,256,8]{2,1,3,0:T(8,128)(2,1)}, bf16[4,128,256,8]{2,1,3,0:T(8,128)(2,1)S(1)}, u32[]{:S(2)}) copy-start(bf16[4,128,256,8]{2,1,3,0:T(8,128)(2,1)S(1)} %fusion.6) | copy-start | bytes 6291460
  36.3 3.0 %copy-start.12 = (f32[1,32,128]{2,1,0:T(8,128)}, f32[1,32,128]{2,1,0:T(8,128)S(1)}, u32[]{:S(2)}) copy-start(f32[1,32,128]{2,1,0:T(8,128)S(1)} %get-tuple-element.90) | copy-start | bytes 49156
  37.7 1.7 copy-start.18
  37.7 1.7 copy-start.20
  41.3 1.4 copy-start.17
  42.6 0.7 copy-start.16
  42.6 0.9 copy-start.23
  42.6 1.0 copy-start.22
  42.7 16.0 %copy-start.6 = (bf16[1,2,128,128]{3,2,1,0:T(8,128)(2,1)S(1)}, bf16[1,2,128,128]{3,2,1,0:T(8,128)(2,1)}, u32[]{:S(2)}) copy-start(bf16[1,2,128,128]{3,2,1,0:T(8,128)(2,1)} %maximum_bitcast_fusion.9) | copy-start | bytes 196612
  42.7 16.0 %copy-start.7 = (bf16[1,2,128,128]{3,2,1,0:T(8,128)(2,1)S(1)}, bf16[1,2,128,128]{3,2,1,0:T(8,128)(2,1)}, u32[]{:S(2)}) copy-start(bf16[1,2,128,128]{3,2,1,0:T(8,128)(2,1)} %maximum_bitcast_fusion.6) | copy-start | bytes 196612
  42.7 16.0 %copy-start.8 = (bf16[1,2,128,128]{3,2,1,0:T(8,128)(2,1)S(1)}, bf16[1,2,128,128]{3,2,1,0:T(8,128)(2,1)}, u32[]{:S(2)}) copy-start(bf16[1,2,128,128]{3,2,1,0:T(8,128)(2,1)} %maximum_bitcast_fusion.8) | copy-start | bytes 196612
  44.5 36.8 %all-to-all-start.1 = ((bf16[4,528,128]{2,1,0:T(8,128)(2,1)}), bf16[4,528,128]{2,1,0:T(8,128)(2,1)S(1)}, u32[]{:S(2)}, u32[]{:S(2)}) async-start(bf16[4,528,128]{2,1,0:T(8,128)(2,1)} %pad_maximum_fusion.3), calls=%async_computation.1 | async-start | bytes 1081344 | tf_op jit(solution)/shard_map/all_to_all | solution.py:42
  58.9 6.8 %copy-start.4 = (bf16[1024,2,128]{2,0,1:T(8,128)(2,1)S(1)}, bf16[1024,2,128]{2,0,1:T(8,128)(2,1)}, u32[]{:S(2)}) copy-start(bf16[1024,2,128]{2,0,1:T(8,128)(2,1)} %copy-done.3) | copy-start | bytes 1572868
  81.4 7.6 %copy-start.26 = (f32[32]{0:T(128)S(1)}, f32[32]{0:T(128)}, u32[]{:S(2)}) copy-start(f32[32]{0:T(128)} %get-tuple-element.27) | copy-start | bytes 388
  81.5 22.0 %copy-start.21 = (f32[2,16]{1,0:T(2,128)S(1)}, f32[2,16]{1,0:T(2,128)}, u32[]{:S(2)}) copy-start(f32[2,16]{1,0:T(2,128)} %copy-done.20) | copy-start | bytes 388
  81.6 22.0 %copy-start.19 = (f32[2,16]{1,0:T(2,128)S(1)}, f32[2,16]{1,0:T(2,128)}, u32[]{:S(2)}) copy-start(f32[2,16]{1,0:T(2,128)} %copy-done.18) | copy-start | bytes 388
  82.5 21.0 %all-to-all-start.2 = ((bf16[4,512,128]{2,1,0:T(8,128)(2,1)}), bf16[4,512,128]{2,1,0:T(8,128)(2,1)S(1)}, u32[]{:S(2)}, u32[]{:S(2)}) async-start(bf16[4,512,128]{2,1,0:T(8,128)(2,1)} %bitcast.66), calls=%async_computation.2 | async-start | bytes 1048576 | tf_op jit(solution)/shard_map/all_to_all | solution.py:55
  103.4 1.0 copy-start.5
  103.6 1.5 copy-start.27
  104.8 1.0 copy-start.28
  105.1 1.0 copy-start.14
  105.1 1.0 copy-start.15
  105.2 1.3 copy-start.29
  106.1 1.2 copy-start.11
  106.1 1.2 copy-start.9
  106.1 1.2 copy-start.10
  106.4 1.2 copy-start.13
  107.1 18.9 %copy-start.1 = (bf16[4,128,256,8]{2,1,3,0:T(8,128)(2,1)S(1)}, bf16[4,128,256,8]{2,1,3,0:T(8,128)(2,1)}, u32[]{:S(2)}) copy-start(bf16[4,128,256,8]{2,1,3,0:T(8,128)(2,1)} %copy-done) | copy-start | bytes 6291460
  107.8 39.4 %collective-permute-start.2 = (bf16[1536,128]{1,0:T(8,128)(2,1)S(1)}, bf16[1536,128]{1,0:T(8,128)(2,1)S(1)}, u32[]{:S(2)}, u32[]{:S(2)}) collective-permute-start(bf16[1536,128]{1,0:T(8,128)(2,1)S(1)} %get-tuple-element.33), channel_id=1, source_target_pairs={{0,1},{1,0},{2,3},{3,2},{4,5},{5,4},{6,7},{7,6},{8,9},{9,8},{10,11... | collective-permute-start | bytes 1179656 | tf_op jit(solution)/shard_map/ppermute | solution.py:19
  127.5 33.0 %all-to-all-start.3 = ((bf16[128,8,128]{2,1,0:T(8,128)(2,1)}), bf16[128,8,128]{2,1,0:T(8,128)(2,1)S(1)}, u32[]{:S(2)}, u32[]{:S(2)}) async-start(bf16[128,8,128]{2,1,0:T(8,128)(2,1)} %fusion.16), calls=%async_computation.3 | async-start | bytes 524288 | tf_op jit(solution)/shard_map/all_to_all | solution.py:210
  161.2 17.7 %all-to-all-start.4 = ((f32[8,8,128]{2,1,0:T(8,128)}), f32[8,8,128]{2,1,0:T(8,128)S(1)}, u32[]{:S(2)}, u32[]{:S(2)}) async-start(f32[8,8,128]{2,1,0:T(8,128)} %broadcast_in_dim.65), calls=%async_computation.4 | async-start | bytes 65536 | tf_op jit(solution)/shard_map/all_to_all | solution.py:24

commit v2 on v1

--- a/solution.py
+++ b/solution.py
@@ -1,6 +1,7 @@
 import jax
 import jax.numpy as jnp
 from jax import lax
+from jax.experimental import pallas as pl
 from jax.sharding import Mesh
 from jax.sharding import PartitionSpec as P
 
@@ -54,6 +55,60 @@
     tiles = pair.astype(BF16).reshape(chips, 2 * rows, STATE)
     tiles = lax.all_to_all(tiles, "chip", 0, 0, tiled=True)
     return tiles[:, :rows].reshape(forward.shape), tiles[:, rows:].reshape(forward.shape)
+
+
+def after_trade(
+    entry_ref, later_ref, forward_ref, backward_ref, decay_ref, tail_ref, leading_ref, step_ref,
+    change_ref, raw_ref, rate_ref, x_ref, dy_ref, bin_ref, bout_ref, through_ref,
+    entry_out, later_out, grad_x_out, grad_raw_out,
+):
+    _, groups, heads, length = tail_ref.shape
+    row = lax.broadcasted_iota(jnp.int32, (length, length), 0)
+    column = lax.broadcasted_iota(jnp.int32, (length, length), 1)
+    from_here = (row >= column).astype(F32)
+    before = 1.0 - from_here
+
+    def by_head(v):
+        return v.reshape(heads, v.shape[0] // heads, v.shape[1])
+
+    def product(a, b):
+        return lax.dot_general(a, b, (((1,), (1,)), ((), ())), preferred_element_type=F32)
+
+    def summed(a, b):
+        return lax.dot_general(
+            a, b, (((1,), (0,)), ((), ())), precision=HIGH, preferred_element_type=F32
+        )
+
+    for b in range(CORES):
+        for g in range(groups):
+            entry, later = entry_ref[g], later_ref[g]
+            if b == 1:
+                carried_in = by_head(entry.astype(F32)) * decay_ref[0, g][:, :, None]
+                entry = forward_ref[g] + carried_in.reshape(entry.shape)
+                entry = entry.astype(BF16)
+            else:
+                carried_in = by_head(later.astype(F32)) * decay_ref[1, g][:, :, None]
+                later = backward_ref[g] + carried_in.reshape(later.shape)
+                later = later.astype(BF16)
+            entry_out[b, g] = entry
+            later_out[b, g] = later
+            carried = by_head(product(later, bin_ref[b, g]))
+            read = by_head(product(entry, bout_ref[b, g]))
+            tail, step = tail_ref[b, g], step_ref[b, g]
+            x = by_head(x_ref[b, g].astype(F32))
+            dy = by_head(dy_ref[b, g].astype(F32))
+            inner = by_head(through_ref[b, g]) + tail[:, None, :] * carried
+            grad_x = step[:, None, :] * inner
+            grad_x_out[b, g] = grad_x.reshape(x_ref.shape[2:]).astype(BF16)
+            direct = jnp.sum(x * inner, axis=1)
+            entry_term = leading_ref[b, g] * jnp.sum(read * dy, axis=1)
+            exit_term = tail * step * jnp.sum(x * carried, axis=1)
+            both = by_head(later.astype(F32) * entry.astype(F32))
+            closing = decay_ref[b, g] * jnp.sum(jnp.sum(both, axis=1), axis=1, keepdims=True)
+            grad_log = summed(change_ref[b, g] + entry_term, from_here) + summed(exit_term, before)
+            grad_step = direct - rate_ref[g] * (grad_log + closing)
+            grad_raw = grad_step * jax.nn.sigmoid(raw_ref[b, g])
+            grad_raw_out[b, g] = grad_raw.astype(BF16)
 
 
 def body(
@@ -178,28 +233,34 @@
         together,
     )
     through, change, local_b, local_c = local
-    entry = entry.reshape(forward.shape[1:])
-    later = later.reshape(forward.shape[1:])
-    entry = jnp.stack([entry, (forward[0] + factor[0] * entry).astype(BF16)])
-    later = jnp.stack([(backward[1] + factor[1] * later).astype(BF16), later])
-
-    carried = jnp.einsum("bgkpn,bgsn->bgkps", later, bin_half, preferred_element_type=F32)
-    read = jnp.einsum("bgkpn,bgtn->bgkpt", entry, bout_half, preferred_element_type=F32)
-    inner_x = through + tail[..., None, :] * carried
-    direct = jnp.sum(inputs * inner_x, axis=3)
-    entry_term = leading * jnp.sum(read * upstream, axis=3)
-    exit_term = tail * step_grid * jnp.sum(inputs * carried, axis=3)
-    closing = block_decay[..., 0] * jnp.sum(
-        later.astype(F32) * entry.astype(F32), axis=(3, 4)
-    )
-    grad_cum = jnp.concatenate([change + entry_term, exit_term], axis=-1)
-    sums = jnp.concatenate([triangle, 1.0 - triangle])
-    grad_log = jnp.dot(grad_cum.reshape(CORES * heads, -1), sums, precision=HIGH)
-    grad_log = grad_log.reshape(grid) + closing[..., None]
-    grad_step = direct - rate.reshape(groups, per_group, 1) * grad_log
-    grad_raw = grad_step.reshape(raw.shape) * jax.nn.sigmoid(raw)
-
-    grad_raw = jnp.where(upper, grad_raw[::-1], grad_raw).astype(BF16)
+    tall = (CORES, groups, per_group * head_size, LANES)
+    entry, later, grad_x, grad_raw = pl.pallas_call(
+        after_trade,
+        out_shape=[jax.ShapeDtypeStruct(tall, BF16)] * 3 + [jax.ShapeDtypeStruct(grid, BF16)],
+        cost_estimate=pl.CostEstimate(flops=2**29, bytes_accessed=2**23, transcendentals=2**13),
+    )(
+        entry.reshape(tall[1:]),
+        later.reshape(tall[1:]),
+        forward[0].reshape(tall[1:]),
+        backward[1].reshape(tall[1:]),
+        block_decay,
+        tail,
+        leading,
+        step_grid,
+        change,
+        raw.reshape(grid),
+        rate.reshape(groups, per_group, 1),
+        x_half.reshape(tall),
+        dy_half.reshape(tall),
+        bin_half,
+        bout_half,
+        through.reshape(tall),
+    )
+    entry = entry.reshape(x_half.shape[:-1] + (STATE,))
+    later = later.reshape(entry.shape)
+    grad_raw = grad_raw.reshape(raw.shape)
+
+    grad_raw = jnp.where(upper, grad_raw[::-1], grad_raw)
     grad_raw = jnp.concatenate([grad_raw[0], grad_raw[1]], axis=1)
     zero = jnp.zeros_like(grad_raw)
     placed = jnp.stack(
@@ -209,7 +270,6 @@
     tiles = partial.astype(BF16).reshape(devices, rows, LANES)
     tiles = lax.all_to_all(tiles, "fsdp", 0, 0, tiled=True)
 
-    grad_x = (step_grid[..., None, :] * inner_x).astype(BF16)
     grad_b = jnp.einsum("bgkps,bgkpn->bgsn", tailed, later, preferred_element_type=F32)
     grad_b = (local_b + grad_b).astype(BF16)
     grad_c = jnp.einsum("bgkpt,bgkpn->bgtn", led, entry, preferred_element_type=F32)

time: 181 us -> 181 us (level)
  waiting for transfers between devices: 48.5 us -> 65.6 us
  starting transfers between devices: 88.4 us -> 75.6 us
  other arithmetic: 14.5 us -> 9.19 us
  Pallas kernels: 0 us -> 4.33 us
  matrix products: 18.5 us -> 15.4 us
    all_to_all x2, starting transfers between devices: 23.5 us -> 13.3 us  [copies_to(): return lax.all_to_all(tiles, axis, 0, 0, tiled=True)]
    all_to_all x1, waiting for transfers between devices: 12.7 us -> 19.9 us  [carried_states(): tiles = together(lax.all_to_all(tiles, 'chip', 0, 0, tiled=True))]
    all_to_all x2, waiting for transfers between devices: 11.3 us -> 17.7 us  [copies_to(): return lax.all_to_all(tiles, axis, 0, 0, tiled=True)]
    pallas_call x0 -> x1, Pallas kernels: none -> 4.33 us  [body(): pl.pallas_call(after_trade, out_shape=[jax.ShapeDtypeStruct(tall, BF16)]...]
    all_to_all x1, waiting for transfers between devices: 13.1 us -> 16 us  [carried_states(): tiles = lax.all_to_all(tiles, 'chip', 0, 0, tiled=True)]
  transfers between devices with their start and end apart: 8 -> 8, of which waited for: 4 -> 6; matrix products, arithmetic and copies ran while one was open for 13% -> 10% of each run, Pallas kernels for 0% -> 0%
where the time goes in v2:
time: 181 us; the launch traced here: 180 us
  starting transfers between devices  75.6 us (42%)
  waiting for transfers between devices  65.6 us (36%)
  matrix products  15.4 us (9%)
  other arithmetic  9.19 us (5%)
  local copies, waits for them, and re-layouts  8.74 us (5%)
  Pallas kernels  4.33 us (2%)
    ppermute x3, starting transfers between devices, core_swap(): return lax.ppermute(value, 'core', [(0, 1), (1, 0)])  24.5 us
    all_to_all x1, waiting for transfers between devices, carried_states(): tiles = together(lax.all_to_all(tiles, 'chip', 0, 0, tiled=True))  19.9 us
    all_to_all x1, starting transfers between devices, body(): tiles = lax.all_to_all(tiles, 'fsdp', 0, 0, tiled=True)  18.9 us
    all_to_all x2, waiting for transfers between devices, copies_to(): return lax.all_to_all(tiles, axis, 0, 0, tiled=True)  17.7 us
    all_to_all x1, waiting for transfers between devices, carried_states(): tiles = lax.all_to_all(tiles, 'chip', 0, 0, tiled=True)  16 us
    all_to_all x2, starting transfers between devices, copies_to(): return lax.all_to_all(tiles, axis, 0, 0, tiled=True)  13.3 us
    all_to_all x1, starting transfers between devices, carried_states(): tiles = together(lax.all_to_all(tiles, 'chip', 0, 0, tiled=True))  12.7 us
    all_to_all x1, waiting for transfers between devices, body(): tiles = lax.all_to_all(tiles, 'fsdp', 0, 0, tiled=True)  11.4 us
  transfers between devices with their start and end apart: 8, of which 6 were waited for; matrix products, arithmetic and copies ran while one was open for 10% of the time, Pallas kernels for 0%

profile of v2, /device:TPU:1, one launch (start us, length us, event | category | flops | bytes accessed | tf_op | source)
XLA Modules:
  0.0 180.4 jit_solution(13521261641882954405)
XLA Ops:
  0.7 1.4 select_bitcast_fusion.2
  2.2 16.0 %collective-permute-start.1 = (bf16[128,2560]{1,0:T(8,128)(2,1)S(1)}, bf16[128,2560]{1,0:T(8,128)(2,1)S(1)}, u32[]{:S(2)}, u32[]{:S(2)}) collective-permute-start(bf16[128,2560]{1,0:T(8,128)(2,1)S(1)} %pad_maximum_fusion.2), channel_id=1, source_target_pairs={{0,1},{1,0},{2,3},{3,2},{4,5},{5,4},{6,7},{7,6},{8,9},{9,8},{10,11... | collective-permute-start | bytes 1966088 | tf_op jit(solution)/shard_map/ppermute | solution.py:20
  18.4 0.8 broadcast_in_dim.28
  19.1 7.3 %all-to-all-start = ((bf16[128,8,128]{2,1,0:T(8,128)(2,1)}), bf16[128,8,128]{2,1,0:T(8,128)(2,1)}, u32[]{:S(2)}, u32[]{:S(2)}) async-start(bf16[128,8,128]{2,1,0:T(8,128)(2,1)} %broadcast_in_dim.28), calls=%async_computation | async-start | bytes 524288 | tf_op jit(solution)/shard_map/all_to_all | solution.py:25
  26.4 1.9 %collective-permute-start = (bf16[128,4096]{1,0:T(8,128)(2,1)S(1)}, bf16[128,4096]{1,0:T(8,128)(2,1)S(1)}, u32[]{:S(2)}, u32[]{:S(2)}) collective-permute-start(bf16[128,4096]{1,0:T(8,128)(2,1)S(1)} %bitcast.243), channel_id=1, source_target_pairs={{0,1},{1,0},{2,3},{3,2},{4,5},{5,4},{6,7},{7,6},{8,9},{9,8},{10,11... | collective-permute-start | bytes 3145736 | tf_op jit(solution)/shard_map/ppermute | solution.py:20
  28.8 0.8 fusion.1
  29.6 0.8 fusion.3
  30.4 0.6 collective-permute-done
  31.2 0.9 copy.47
  32.1 1.4 fusion.6
  33.5 6.4 %all-to-all-done = bf16[128,8,128]{2,1,0:T(8,128)(2,1)} async-done(((bf16[128,8,128]{2,1,0:T(8,128)(2,1)}), bf16[128,8,128]{2,1,0:T(8,128)(2,1)}, u32[]{:S(2)}, u32[]{:S(2)}) %all-to-all-start) | async-done | bytes 262176 | tf_op jit(solution)/shard_map/all_to_all | solution.py:25
  39.9 1.4 convolution_bitcast_fusion.1
  41.4 0.2 fusion.51
  42.0 0.6 compare_select_fusion
  42.6 0.7 fusion.89
  43.3 0.6 copy-done.20
  43.9 0.3 fusion.35
  44.2 0.9 fusion.91
  45.5 0.3 fusion.36
  46.6 0.2 add_convert_fusion
  47.0 0.9 pad_maximum_fusion.3
  47.9 12.7 %all-to-all-start.1 = ((bf16[4,528,128]{2,1,0:T(8,128)(2,1)}), bf16[4,528,128]{2,1,0:T(8,128)(2,1)S(1)}, u32[]{:S(2)}, u32[]{:S(2)}) async-start(bf16[4,528,128]{2,1,0:T(8,128)(2,1)} %pad_maximum_fusion.3), calls=%async_computation.1 | async-start | bytes 1081344 | tf_op jit(solution)/shard_map/all_to_all | solution.py:43
  60.6 0.2 fusion.99
  60.9 3.6 %multiply_reduce_fusion = (f32[2,2,16,128]{3,2,1,0:T(8,128)S(1)}, f32[2,2,16,128]{3,2,1,0:T(8,128)S(1)}, bf16[2,2,128,128]{3,2,1,0:T(8,128)(2,1)S(1)}) fusion(f32[2,2,128,128]{3,2,1,0:T(8,128)S(1)} %fusion.99, f32[2,2,16,128]{3,2,1,0:T(8,128)S(1)} %copy-done.19, bf16[2,2,16,32,128]{4,3,2,1,0:T(8,128)(2,1)S(1)} %bitcast.234, ...), kind=kOutput, calls=%fused_computation.7 | convolution fusion | flops 76464128 | bytes 1589248 | tf_op jit(solution)/shard_map/bgkpt,bgkps->bgkts/dot_general | solution.py:214
  64.5 0.6 sub.54.change_ref
  65.3 0.2 fusion.101
  65.5 2.8 %fusion.5 = f32[2,2,16,32,128]{4,3,2,1,0:T(8,128)} fusion(bf16[2,2,16,32,128]{4,3,2,1,0:T(8,128)(2,1)S(1)} %bitcast.235, f32[2,2,128,128]{3,2,1,0:T(8,128)S(1)} %fusion.99, f32[2,2,16,128]{3,2,1,0:T(8,128)S(1)} %bitcast.261, pred[128,128]{1,0:T(8,128)(4,1)S(1)} %iota_compare_fusion.2), kind=kOutput, calls=%fused_computation.9 | convolution fusion | flops 72351744 | bytes 1884160 | tf_op jit(solution)/shard_map/bgkpt,bgkts->bgkps/dot_general | solution.py:215
  68.4 19.9 %all-to-all-done.1 = bf16[4,528,128]{2,1,0:T(8,128)(2,1)S(1)} async-done(((bf16[4,528,128]{2,1,0:T(8,128)(2,1)}), bf16[4,528,128]{2,1,0:T(8,128)(2,1)S(1)}, u32[]{:S(2)}, u32[]{:S(2)}) %all-to-all-start.1) | async-done | bytes 540704 | tf_op jit(solution)/shard_map/all_to_all | solution.py:43
  88.6 0.8 pad_maximum_fusion.4
  89.5 6.2 %all-to-all-start.2 = ((bf16[4,512,128]{2,1,0:T(8,128)(2,1)}), bf16[4,512,128]{2,1,0:T(8,128)(2,1)S(1)}, u32[]{:S(2)}, u32[]{:S(2)}) async-start(bf16[4,512,128]{2,1,0:T(8,128)(2,1)} %bitcast.66), calls=%async_computation.2 | async-start | bytes 1048576 | tf_op jit(solution)/shard_map/all_to_all | solution.py:56
  95.7 0.7 select_n.281.rate_ref
  96.4 16.0 %all-to-all-done.2 = bf16[4,512,128]{2,1,0:T(8,128)(2,1)S(1)} async-done(((bf16[4,512,128]{2,1,0:T(8,128)(2,1)}), bf16[4,512,128]{2,1,0:T(8,128)(2,1)S(1)}, u32[]{:S(2)}, u32[]{:S(2)}) %all-to-all-start.2) | async-done | bytes 524320 | tf_op jit(solution)/shard_map/all_to_all | solution.py:56
  112.4 0.8 fusion.93
  113.2 4.3 %shard_map.111 = (bf16[2,2,512,128]{3,2,1,0:T(8,128)(2,1)}, bf16[2,2,512,128]{3,2,1,0:T(8,128)(2,1)}, bf16[2,2,512,128]{3,2,1,0:T(8,128)(2,1)}, bf16[2,2,16,128]{3,2,1,0:T(8,128)(2,1)}) custom-call(bf16[2,512,128]{2,1,0:T(8,128)(2,1)} %bitcast.242, bf16[2,512,128]{2,1,0:T(8,128)(2,1)} %bitcast.241, f32[2,512,128]{2,1,0:T(8,128)} %bitcast.223, ...), custom_call_target="tpu_custom_call" | custom-call | flops 536870912 | bytes 8388608 | tf_op jit(solution)/shard_map/pallas_call | solution.py:237
  117.6 0.8 reverse_select_fusion
  118.5 1.4 fusion.19
  120.0 0.4 fusion.18
  120.5 6.6 %collective-permute-start.2 = (bf16[1536,128]{1,0:T(8,128)(2,1)S(1)}, bf16[1536,128]{1,0:T(8,128)(2,1)S(1)}, u32[]{:S(2)}, u32[]{:S(2)}) collective-permute-start(bf16[1536,128]{1,0:T(8,128)(2,1)S(1)} %get-tuple-element.39), channel_id=1, source_target_pairs={{0,1},{1,0},{2,3},{3,2},{4,5},{5,4},{6,7},{7,6},{8,9},{9,8},{10,11... | collective-permute-start | bytes 1179656 | tf_op jit(solution)/shard_map/ppermute | solution.py:20
  127.1 1.4 fusion.15
  128.5 18.9 %all-to-all-start.3 = ((bf16[128,8,128]{2,1,0:T(8,128)(2,1)}), bf16[128,8,128]{2,1,0:T(8,128)(2,1)S(1)}, u32[]{:S(2)}, u32[]{:S(2)}) async-start(bf16[128,8,128]{2,1,0:T(8,128)(2,1)} %fusion.15), calls=%async_computation.3 | async-start | bytes 524288 | tf_op jit(solution)/shard_map/all_to_all | solution.py:271
  147.6 1.0 copy.45
  148.7 0.7 maximum_bitcast_fusion.3
  149.4 11.4 %all-to-all-done.3 = bf16[128,8,128]{2,1,0:T(8,128)(2,1)S(1)} async-done(((bf16[128,8,128]{2,1,0:T(8,128)(2,1)}), bf16[128,8,128]{2,1,0:T(8,128)(2,1)S(1)}, u32[]{:S(2)}, u32[]{:S(2)}) %all-to-all-start.3) | async-done | bytes 262176 | tf_op jit(solution)/shard_map/all_to_all | solution.py:271
  160.9 0.6 broadcast_in_dim.63
  161.5 6.0 %all-to-all-start.4 = ((f32[8,8,128]{2,1,0:T(8,128)}), f32[8,8,128]{2,1,0:T(8,128)S(1)}, u32[]{:S(2)}, u32[]{:S(2)}) async-start(f32[8,8,128]{2,1,0:T(8,128)} %broadcast_in_dim.63), calls=%async_computation.4 | async-start | bytes 65536 | tf_op jit(solution)/shard_map/all_to_all | solution.py:25
  167.5 0.7 maximum_bitcast_fusion.2
  168.2 11.3 %all-to-all-done.4 = f32[8,8,128]{2,1,0:T(8,128)S(1)} async-done(((f32[8,8,128]{2,1,0:T(8,128)}), f32[8,8,128]{2,1,0:T(8,128)S(1)}, u32[]{:S(2)}, u32[]{:S(2)}) %all-to-all-start.4) | async-done | bytes 32800 | tf_op jit(solution)/shard_map/all_to_all | solution.py:25
  179.7 0.7 reshape.411
  (126 shorter events, 3.7 us)
Async XLA Ops:
  0.6 1.4 copy-start.23
  0.6 1.4 copy-start.22
  0.7 17.6 %copy-start.24 = (bf16[32,64]{1,0:T(8,128)(2,1)S(1)}, bf16[32,64]{1,0:T(8,128)(2,1)}, u32[]{:S(2)}) copy-start(bf16[32,64]{1,0:T(8,128)(2,1)} %param.9) | copy-start | bytes 12292
  0.7 25.7 %copy-start.13 = (bf16[1,128,4096]{2,1,0:T(8,128)(2,1)S(1)}, bf16[1,128,4096]{2,1,0:T(8,128)(2,1)}, u32[]{:S(2)}) copy-start(bf16[1,128,4096]{2,1,0:T(8,128)(2,1)} %param.8) | copy-start | bytes 3145732
  2.0 26.4 %copy-start.25 = (f32[64]{0:T(128)S(1)}, f32[64]{0:T(128)}, u32[]{:S(2)}) copy-start(f32[64]{0:T(128)} %param.10) | copy-start | bytes 772
  2.1 26.5 %copy-start.26 = (f32[64]{0:T(128)S(1)}, f32[64]{0:T(128)}, u32[]{:S(2)}) copy-start(f32[64]{0:T(128)} %param.11) | copy-start | bytes 772
  2.2 26.4 %collective-permute-start.1 = (bf16[128,2560]{1,0:T(8,128)(2,1)S(1)}, bf16[128,2560]{1,0:T(8,128)(2,1)S(1)}, u32[]{:S(2)}, u32[]{:S(2)}) collective-permute-start(bf16[128,2560]{1,0:T(8,128)(2,1)S(1)} %pad_maximum_fusion.2), channel_id=1, source_target_pairs={{0,1},{1,0},{2,3},{3,2},{4,5},{5,4},{6,7},{7,6},{8,9},{9,8},{10,11... | collective-permute-start | bytes 1966088 | tf_op jit(solution)/shard_map/ppermute | solution.py:20
  19.1 20.8 %all-to-all-start = ((bf16[128,8,128]{2,1,0:T(8,128)(2,1)}), bf16[128,8,128]{2,1,0:T(8,128)(2,1)}, u32[]{:S(2)}, u32[]{:S(2)}) async-start(bf16[128,8,128]{2,1,0:T(8,128)(2,1)} %broadcast_in_dim.28), calls=%async_computation | async-start | bytes 524288 | tf_op jit(solution)/shard_map/all_to_all | solution.py:25
  26.4 4.6 %collective-permute-start = (bf16[128,4096]{1,0:T(8,128)(2,1)S(1)}, bf16[128,4096]{1,0:T(8,128)(2,1)S(1)}, u32[]{:S(2)}, u32[]{:S(2)}) collective-permute-start(bf16[128,4096]{1,0:T(8,128)(2,1)S(1)} %bitcast.243), channel_id=1, source_target_pairs={{0,1},{1,0},{2,3},{3,2},{4,5},{5,4},{6,7},{7,6},{8,9},{9,8},{10,11... | collective-permute-start | bytes 3145736 | tf_op jit(solution)/shard_map/ppermute | solution.py:20
  28.7 36.4 %copy-start.2 = (bf16[2,2,128,128]{3,2,1,0:T(8,128)(2,1)}, bf16[2,2,128,128]{3,2,1,0:T(8,128)(2,1)S(1)}, u32[]{:S(2)}) copy-start(bf16[2,2,128,128]{3,2,1,0:T(8,128)(2,1)S(1)} %maximum_select_fusion.5.bin_ref) | copy-start | bytes 393220
  29.5 16.0 %copy-start.7 = (bf16[1024,2,128]{2,0,1:T(8,128)(2,1)}, bf16[1024,2,128]{2,0,1:T(8,128)(2,1)S(1)}, u32[]{:S(2)}) copy-start(bf16[1024,2,128]{2,0,1:T(8,128)(2,1)S(1)} %fusion.1) | copy-start | bytes 1572868
  29.6 35.7 %copy-start.3 = (bf16[2,2,128,128]{3,2,1,0:T(8,128)(2,1)}, bf16[2,2,128,128]{3,2,1,0:T(8,128)(2,1)S(1)}, u32[]{:S(2)}) copy-start(bf16[2,2,128,128]{3,2,1,0:T(8,128)(2,1)S(1)} %maximum_select_fusion.6.bout_ref) | copy-start | bytes 393220
  30.4 13.0 %copy-start.10 = (bf16[1024,2,128]{2,0,1:T(8,128)(2,1)}, bf16[1024,2,128]{2,0,1:T(8,128)(2,1)S(1)}, u32[]{:S(2)}) copy-start(bf16[1024,2,128]{2,0,1:T(8,128)(2,1)S(1)} %fusion.3) | copy-start | bytes 1572868
  33.5 10.8 %copy-start.4 = (bf16[4,128,256,8]{2,1,3,0:T(8,128)(2,1)}, bf16[4,128,256,8]{2,1,3,0:T(8,128)(2,1)S(1)}, u32[]{:S(2)}) copy-start(bf16[4,128,256,8]{2,1,3,0:T(8,128)(2,1)S(1)} %fusion.6) | copy-start | bytes 6291460
  41.8 3.6 %copy-start.17 = (f32[2,2,16,1]{3,2,1,0:T(8,128)}, f32[2,2,16,1]{3,2,1,0:T(8,128)S(1)}, u32[]{:S(2)}) copy-start(f32[2,2,16,1]{3,2,1,0:T(8,128)S(1)} %get-tuple-element.93.decay_ref) | copy-start | bytes 772
  42.6 3.2 %copy-start.18 = (f32[2,2,16,128]{3,2,1,0:T(8,128)}, f32[2,2,16,128]{3,2,1,0:T(8,128)S(1)}, u32[]{:S(2)}) copy-start(f32[2,2,16,128]{3,2,1,0:T(8,128)S(1)} %get-tuple-element.28.raw_ref) | copy-start | bytes 98308
  43.3 0.6 copy-start.20
  43.3 2.5 %copy-start.15 = (f32[2,2,16,128]{3,2,1,0:T(8,128)}, f32[2,2,16,128]{3,2,1,0:T(8,128)S(1)}, u32[]{:S(2)}) copy-start(f32[2,2,16,128]{3,2,1,0:T(8,128)S(1)} %get-tuple-element.91.leading_ref) | copy-start | bytes 98308
  45.2 1.4 copy-start
  45.2 1.2 copy-start.6
  45.9 2.0 %copy-start.1 = (f32[1,2,16,32,128]{4,3,2,1,0:T(8,128)}, f32[1,2,16,32,128]{4,3,2,1,0:T(8,128)S(1)}, u32[]{:S(2)}) copy-start(f32[1,2,16,32,128]{4,3,2,1,0:T(8,128)S(1)} %get-tuple-element.37) | copy-start | bytes 1572868
  46.6 14.2 %copy-start.8 = (bf16[1024,2,128]{2,0,1:T(8,128)(2,1)S(1)}, bf16[1024,2,128]{2,0,1:T(8,128)(2,1)}, u32[]{:S(2)}) copy-start(bf16[1024,2,128]{2,0,1:T(8,128)(2,1)} %copy-done.7) | copy-start | bytes 1572868
  46.6 14.2 %copy-start.11 = (bf16[1024,2,128]{2,0,1:T(8,128)(2,1)S(1)}, bf16[1024,2,128]{2,0,1:T(8,128)(2,1)}, u32[]{:S(2)}) copy-start(bf16[1024,2,128]{2,0,1:T(8,128)(2,1)} %copy-done.10) | copy-start | bytes 1572868
  46.6 14.2 %copy-start.19 = (f32[2,2,16,128]{3,2,1,0:T(8,128)S(1)}, f32[2,2,16,128]{3,2,1,0:T(8,128)}, u32[]{:S(2)}) copy-start(f32[2,2,16,128]{3,2,1,0:T(8,128)} %get-tuple-element.27.step_ref) | copy-start | bytes 98308
  47.9 40.4 %all-to-all-start.1 = ((bf16[4,528,128]{2,1,0:T(8,128)(2,1)}), bf16[4,528,128]{2,1,0:T(8,128)(2,1)S(1)}, u32[]{:S(2)}, u32[]{:S(2)}) async-start(bf16[4,528,128]{2,1,0:T(8,128)(2,1)} %pad_maximum_fusion.3), calls=%async_computation.1 | async-start | bytes 1081344 | tf_op jit(solution)/shard_map/all_to_all | solution.py:43
  89.5 22.9 %all-to-all-start.2 = ((bf16[4,512,128]{2,1,0:T(8,128)(2,1)}), bf16[4,512,128]{2,1,0:T(8,128)(2,1)S(1)}, u32[]{:S(2)}, u32[]{:S(2)}) async-start(bf16[4,512,128]{2,1,0:T(8,128)(2,1)} %bitcast.66), calls=%async_computation.2 | async-start | bytes 1048576 | tf_op jit(solution)/shard_map/all_to_all | solution.py:56
  113.2 5.2 %copy-start.12 = (bf16[1024,2,128]{2,0,1:T(8,128)(2,1)S(1)}, bf16[1024,2,128]{2,0,1:T(8,128)(2,1)}, u32[]{:S(2)}) copy-start(bf16[1024,2,128]{2,0,1:T(8,128)(2,1)} %copy-done.10) | copy-start | bytes 1572868
  113.2 5.2 %copy-start.21 = (f32[2,2,16,128]{3,2,1,0:T(8,128)S(1)}, f32[2,2,16,128]{3,2,1,0:T(8,128)}, u32[]{:S(2)}) copy-start(f32[2,2,16,128]{3,2,1,0:T(8,128)} %copy-done.20) | copy-start | bytes 98308
  117.6 2.4 %copy-start.9 = (bf16[1024,2,128]{2,0,1:T(8,128)(2,1)S(1)}, bf16[1024,2,128]{2,0,1:T(8,128)(2,1)}, u32[]{:S(2)}) copy-start(bf16[1024,2,128]{2,0,1:T(8,128)(2,1)} %copy-done.7) | copy-start | bytes 1572868
  117.6 2.4 %copy-start.16 = (f32[2,2,16,128]{3,2,1,0:T(8,128)S(1)}, f32[2,2,16,128]{3,2,1,0:T(8,128)}, u32[]{:S(2)}) copy-start(f32[2,2,16,128]{3,2,1,0:T(8,128)} %copy-done.15) | copy-start | bytes 98308
  117.6 2.4 %copy-start.27 = (bf16[2,2,512,128]{3,2,1,0:T(8,128)(2,1)S(1)}, bf16[2,2,512,128]{3,2,1,0:T(8,128)(2,1)}, u32[]{:S(2)}) copy-start(bf16[2,2,512,128]{3,2,1,0:T(8,128)(2,1)} %get-tuple-element.20) | copy-start | bytes 1572868
  118.4 1.9 %copy-start.14 = (bf16[2,2,512,128]{3,2,1,0:T(8,128)(2,1)S(1)}, bf16[2,2,512,128]{3,2,1,0:T(8,128)(2,1)}, u32[]{:S(2)}) copy-start(bf16[2,2,512,128]{3,2,1,0:T(8,128)(2,1)} %get-tuple-element.16) | copy-start | bytes 1572868
  120.3 6.8 %copy-start.5 = (bf16[4,128,256,8]{2,1,3,0:T(8,128)(2,1)S(1)}, bf16[4,128,256,8]{2,1,3,0:T(8,128)(2,1)}, u32[]{:S(2)}) copy-start(bf16[4,128,256,8]{2,1,3,0:T(8,128)(2,1)} %copy-done.4) | copy-start | bytes 6291460
  120.5 27.0 %collective-permute-start.2 = (bf16[1536,128]{1,0:T(8,128)(2,1)S(1)}, bf16[1536,128]{1,0:T(8,128)(2,1)S(1)}, u32[]{:S(2)}, u32[]{:S(2)}) collective-permute-start(bf16[1536,128]{1,0:T(8,128)(2,1)S(1)} %get-tuple-element.39), channel_id=1, source_target_pairs={{0,1},{1,0},{2,3},{3,2},{4,5},{5,4},{6,7},{7,6},{8,9},{9,8},{10,11... | collective-permute-start | bytes 1179656 | tf_op jit(solution)/shard_map/ppermute | solution.py:20
  128.5 32.2 %all-to-all-start.3 = ((bf16[128,8,128]{2,1,0:T(8,128)(2,1)}), bf16[128,8,128]{2,1,0:T(8,128)(2,1)S(1)}, u32[]{:S(2)}, u32[]{:S(2)}) async-start(bf16[128,8,128]{2,1,0:T(8,128)(2,1)} %fusion.15), calls=%async_computation.3 | async-start | bytes 524288 | tf_op jit(solution)/shard_map/all_to_all | solution.py:271
  161.5 18.0 %all-to-all-start.4 = ((f32[8,8,128]{2,1,0:T(8,128)}), f32[8,8,128]{2,1,0:T(8,128)S(1)}, u32[]{:S(2)}, u32[]{:S(2)}) async-start(f32[8,8,128]{2,1,0:T(8,128)} %broadcast_in_dim.63), calls=%async_computation.4 | async-start | bytes 65536 | tf_op jit(solution)/shard_map/all_to_all | solution.py:25
